TPU v7x, 32 devices: a whole 2x2x4 slice. The times are simulated.
32 devices in a mesh: dp: 2 (over x), tp: 16 (over y, z, core).
Axes of the slice: x: 2, y: 2, z: 4, core: 2. Of those that a mesh axis runs over, the one named last changes fastest.
Arguments:
- x: bfloat16 [4096, 8192], P('dp'), parts along dimension 0
- w_gate: bfloat16 [8192, 32768], P(None, 'tp')
- w_up: bfloat16 [8192, 32768], P(None, 'tp')
- w_down: bfloat16 [32768, 8192], P('tp')
Outputs:
- output: bfloat16 [4096, 8192], P('dp'), parts along dimension 0
There are 2 independent parts. A program takes and returns all parts, laid end to end along the dimension named above; an argument that names none is the same for every part.
All inputs are finite; a program needn't handle non-finite values.
Results may differ from a plain program's by a relative error of at most 0.016.
Values are sent between devices in bfloat16 or wider.
A program may use at most 2 GiB of HBM per device.

v0:
```python
import jax
import jax.numpy as jnp
from jax import lax
from jax.sharding import PartitionSpec as P


def solution(mesh):
    def step(x, w_gate, w_up, w_down):
        gate = jnp.dot(x, w_gate, preferred_element_type=jnp.float32)
        up = jnp.dot(x, w_up, preferred_element_type=jnp.float32)
        hidden = (jax.nn.silu(gate) * up).astype(jnp.bfloat16)
        term = jnp.dot(hidden, w_down, preferred_element_type=jnp.float32).astype(jnp.bfloat16)
        return lax.psum(term, "tp")

    return jax.shard_map(
        step,
        mesh=mesh,
        in_specs=(P("dp", None), P(None, "tp"), P(None, "tp"), P("tp", None)),
        out_specs=P("dp", None),
        check_vma=False,
    )
```

profile of v0, /device:TPU:0, one launch (start us, length us, event | category | flops | bytes accessed | tf_op | source)
XLA Modules:
  0.0 843.8 jit_solution(6625874622637878470)
XLA Ops:
  6.5 0.0 all-reduce.2.cloned.1.call-start
  6.5 79.3 %fusion = f32[2048,2048]{1,0:T(8,128)} fusion(bf16[2048,8192]{1,0:T(8,128)(2,1)} %param.4, bf16[8192,2048]{1,0:T(8,128)(2,1)} %param.5), kind=kOutput, calls=%fused_computation.2 | convolution fusion | flops 68719476736 | bytes 83886080 | tf_op jit(solution)/shard_map/dot_general | solution.py:9
  85.8 83.1 %multiply_convert_fusion = bf16[2048,2048]{1,0:T(8,128)(2,1)} fusion(f32[2048,2048]{1,0:T(8,128)} %fusion, bf16[2048,8192]{1,0:T(8,128)(2,1)} %param.4, bf16[8192,2048]{1,0:T(8,128)(2,1)} %param.6), kind=kOutput, calls=%fused_computation.1 | convolution fusion | flops 68744642560 | bytes 92274688 | tf_op jit(solution)/shard_map/dot_general | solution.py:10
  168.9 77.9 %convolution_convert_fusion = bf16[2048,8192]{1,0:T(8,128)(2,1)} fusion(bf16[2048,2048]{1,0:T(8,128)(2,1)} %multiply_convert_fusion, bf16[2048,8192]{1,0:T(8,128)(2,1)} %param.7), kind=kOutput, calls=%fused_computation | convolution fusion | flops 68736253952 | bytes 75497472 | tf_op jit(solution)/shard_map/dot_general | solution.py:12
  246.8 0.0 all-reduce.2.cloned.1.call-update
  246.9 567.1 %all-reduce.2.cloned.1.call-done = bf16[2048,8192]{1,0:T(8,128)(2,1)} async-done(((bf16[2048,8192]{1,0:T(8,128)(2,1)}), bf16[2048,8192]{1,0:T(8,128)(2,1)}) %all-reduce.2.cloned.1.call-update) | async-done | bytes 33554448 | tf_op jit(solution)/shard_map/psum | solution.py:13
  814.0 23.0 %copy.6 = bf16[2048,8192]{1,0:T(8,128)(2,1)} copy(bf16[2048,8192]{1,0:T(8,128)(2,1)} %all-reduce.2.cloned.1.call-done) | data formatting | bytes 67108864
Async XLA Ops:
  6.5 807.4 %all-reduce.2.cloned.1.call-start = ((), (), s32[]{:S(2)}) async-start(), calls=%async_computation | async-start | bytes 67108864 | tf_op jit(solution)/shard_map/psum | solution.py:13
Sparse Core Ops, SparseCore 0:
  247.0 566.9 all-reduce.1
where the time goes:
time: 844 us
  waiting for transfers between devices  567 us (67%)
  matrix products  240 us (28%)
  local copies, waits for them, and re-layouts  23 us (3%)
  between operations  13.4 us (2%)
    psum x1, waiting for transfers between devices, step(): return lax.psum(term, 'tp')  567 us
    dot_general x1, matrix products, step(): up = jnp.dot(x, w_up, preferred_element_type=jnp.float32)  83.1 us
    dot_general x1, matrix products, step(): gate = jnp.dot(x, w_gate, preferred_element_type=jnp.float32)  79.3 us
    dot_general x1, matrix products, step(): jnp.dot(hidden, w_down, preferred_element_type=jnp.float32)  77.9 us
    unnamed x1, local copies, waits for them, and re-layouts  23 us
  transfers between devices with their start and end apart: 1, of which 1 were waited for; matrix products, arithmetic and copies ran while one was open for 0% of the time, Pallas kernels for 0%

commit v1 on v0

v1 whole, which is shorter than its diff:
```python
import jax
import jax.numpy as jnp
from jax import lax
from jax.experimental import pallas as pl
from jax.experimental.pallas import tpu as pltpu
from jax.sharding import PartitionSpec as P

ROWS, D, HID = 2048, 8192, 2048
R = 512
CW = 1024
HALF = D // 2
NQ = HALF // CW
CHUNKS = ROWS // R
PAIRS = CHUNKS * NQ
TN = 256
UNITS = HID // TN
NS = 4
B = 64
SLOTS = 6
LEAD = UNITS // 2
OFF = dict(A1e=3, A1m=6, A2m=9, A3m=11, A3e=15, A4e=16, B1m=4, B2m=8, B3m=10, B4m=14, B5m=13, B6m=17, Ce=23, Cm=22)
NIT = LEAD + PAIRS + (SLOTS - 1 + max(OFF.values())) // SLOTS
F32, BF16 = jnp.float32, jnp.bfloat16


def kernel(x, wg, wu, wd, y, xb, gb, ub, hb, wdb, dsend, drecv, sf, sb, r_ya, r_oa, r_xa, r_ob, r_xb, r_yb,
           s_x, s_w, s_wd, s_ds, s_dr, credit, q_rs, q_ss, q_ga, q_gb, q_f, q_loc, q_fw, q_sib):
    dp, t = lax.axis_index("dp"), lax.axis_index("tp")
    core, z, yy = t % 2, (t // 2) % 4, t // 8
    s = z // 2
    mid = (z == 1) | (z == 2)
    end = (z == 0) | (z == 3)

    def tid(a, b, c):
        return (dp, (a * 4 + b) * 2 + c)

    to_y, to_x, to_s = tid(1 - yy, z, core), tid(yy, 3 - z, core), tid(yy, z, 1 - core)
    to_io = tid(yy, z + 1 - 2 * (z % 2), core)

    def rcopy(src, dst, ssem, rsem, dev):
        return pltpu.make_async_remote_copy(
            src_ref=src, dst_ref=dst, send_sem=ssem, recv_sem=rsem, device_id=dev, device_id_type=pl.DeviceIdType.MESH)

    bar = pltpu.get_barrier_semaphore()
    for dev in (to_y, to_io, to_s):
        pl.semaphore_signal(bar, inc=1, device_id=dev, device_id_type=pl.DeviceIdType.MESH)

    @pl.when(mid)
    def _():
        pl.semaphore_signal(bar, inc=1, device_id=to_x, device_id_type=pl.DeviceIdType.MESH)
        pl.semaphore_wait(bar, 4)

    @pl.when(end)
    def _():
        pl.semaphore_wait(bar, 3)

    def rows(r0, n):
        return pl.ds(pl.multiple_of(r0, B), n)

    def x_copy(c):
        return pltpu.make_async_copy(x.at[rows(c * R, R), :], xb, s_x)

    def w_copies(u):
        b, n = u % 2, pl.ds(pl.multiple_of((u % UNITS) * TN, TN), TN)
        return (pltpu.make_async_copy(wg.at[:, n], gb.at[b], s_w.at[b, 0]),
                pltpu.make_async_copy(wu.at[:, n], ub.at[b], s_w.at[b, 1]))

    def wd_copy(k, half, p):
        n = pl.ds(pl.multiple_of(half * HALF + (p % NQ) * CW, CW), CW)
        return pltpu.make_async_copy(wd.at[:, n], wdb.at[k], s_wd.at[k])

    def gate_up(u, strip):
        b, n = u % 2, pl.ds(pl.multiple_of((u % UNITS) * TN, TN), TN)
        r = pl.ds(strip * (R // 2), R // 2)
        xv = xb[r, :]
        g = jnp.dot(xv, gb[b], preferred_element_type=F32)
        up = jnp.dot(xv, ub[b], preferred_element_type=F32)
        hb[(u // UNITS) % 2, r, n] = (jax.nn.silu(g) * up).astype(BF16)

    def swap(q):
        return rcopy(dsend, drecv.at[q % 2], s_ds, s_dr.at[q % 2], to_s)

    def term_for_other(q):
        for j in range(2):
            n = pl.ds(j * (CW // 2), CW // 2)
            dsend[:, n] = jnp.dot(hb[(q // NQ) % 2], wdb[0, :, n], preferred_element_type=F32).astype(BF16)

    def own_term(p, sl):
        for j in range(2):
            n = pl.ds(j * (CW // 2), CW // 2)
            v = jnp.dot(hb[(p // NQ) % 2], wdb[1, :, n], preferred_element_type=F32) + drecv[p % 2, :, n].astype(F32)
            sf[sl, :, n] = v
            sb[sl, :, n] = v.astype(BF16)

    def add(sl, r0, n, srcs):
        def strip(i, _):
            v = sf[sl, pl.ds(pl.multiple_of(r0 + i * 16, 16), 16), :]
            for ref, q0 in srcs:
                v = v + ref[sl, pl.ds(pl.multiple_of(q0 + i * 16, 16), 16), :].astype(F32)
            sb[sl, pl.ds(pl.multiple_of(r0 + i * 16, 16), 16), :] = v.astype(BF16)
            return 0
        lax.fori_loop(0, n // 16, strip, 0)

    ya, oa, xa, ob, xbl, yb = range(6)

    def reduce_copy(kind, sl, r0, n, dev):
        dst = (r_ya, r_oa, r_xa, r_ob, r_xb, r_yb)[kind].at[sl]
        return rcopy(sb.at[sl, rows(r0, n), :], dst, q_ss.at[sl, kind], q_rs.at[sl, kind], dev)

    def y_at(p, r0, n):
        col = pl.multiple_of(core * HALF + (p % NQ) * CW, CW)
        return y.at[rows((p // NQ) * R + r0, n), pl.ds(col, CW)]

    def block_a(a, b):
        return (a * 2 + b) * B

    def block_b(b, a):
        return 256 + (b * 2 + a) * B

    def recv_sem(sl, r0):
        return q_ga.at[sl, r0 // B]

    def local_final(p, sl, r0, k):
        return pltpu.make_async_copy(sb.at[sl, rows(r0, B), :], y_at(p, r0, B), q_loc.at[sl, k])

    def send_final(p, sl, r0, k, dev):
        return rcopy(sb.at[sl, rows(r0, B), :], y_at(p, r0, B), q_f.at[sl, k], recv_sem(sl, r0), dev)

    def forward(p, sl, r0, k, dev):
        return rcopy(y_at(p, r0, B), y_at(p, r0, B), q_fw.at[sl, k], recv_sem(sl, r0), dev)

    def sibling(p):
        return rcopy(y_at(p, 0, R), y_at(p, 0, R), q_sib.at[0, p], q_sib.at[1, p], to_s)

    def first(p, sl):
        reduce_copy(ya, sl, (1 - yy) * 128, 128, to_y).start()

        @pl.when(end)
        def _():
            reduce_copy(ob, sl, 256, 256, to_io).start()

    def e_a1e(p, sl):
        reduce_copy(ya, sl, 0, 128, to_y).wait_recv()
        add(sl, yy * 128, 128, [(r_ya, 0)])
        reduce_copy(oa, sl, yy * 128, 128, to_io).start()

    def e_a1m(p, sl):
        reduce_copy(ya, sl, 0, 128, to_y).wait_recv()
        reduce_copy(oa, sl, 0, 128, to_io).wait_recv()
        add(sl, block_a(yy, 1 - s), B, [(r_ya, (1 - s) * B), (r_oa, (1 - s) * B)])
        reduce_copy(xa, sl, block_a(yy, 1 - s), B, to_x).start()

    def finals(p, sl, r0, k):
        local_final(p, sl, r0, k).start()
        for i, dev in enumerate((to_io, to_x, to_y)):
            send_final(p, sl, r0, k * 3 + i, dev).start()

    def e_a2m(p, sl):
        reduce_copy(xa, sl, 0, B, to_x).wait_recv()
        add(sl, block_a(yy, s), B, [(r_ya, s * B), (r_oa, s * B), (r_xa, 0)])
        finals(p, sl, block_a(yy, s), 0)

    def arrived(p, sl, r0):
        forward(p, sl, r0, 0, to_y).wait_recv()

    def e_a3m(p, sl):
        r0 = block_a(yy, 1 - s)
        arrived(p, sl, r0)
        forward(p, sl, r0, 0, to_io).start()
        forward(p, sl, r0, 1, to_y).start()

    def e_a3e(p, sl):
        r0 = block_a(yy, s)
        arrived(p, sl, r0)
        forward(p, sl, r0, 0, to_y).start()

    def e_a4e(p, sl):
        r0 = block_a(yy, 1 - s)
        arrived(p, sl, r0)
        forward(p, sl, r0, 1, to_y).start()

    def e_b1m(p, sl):
        reduce_copy(ob, sl, 256, 256, to_io).wait_recv()
        add(sl, block_b(1 - s, 0), 128, [(r_ob, (1 - s) * 128)])
        reduce_copy(xbl, sl, block_b(1 - s, 0), 128, to_x).start()

    def e_b2m(p, sl):
        reduce_copy(xbl, sl, 256, 128, to_x).wait_recv()
        add(sl, block_b(s, 1 - yy), B, [(r_ob, (s * 2 + 1 - yy) * B), (r_xb, (1 - yy) * B)])
        reduce_copy(yb, sl, block_b(s, 1 - yy), B, to_y).start()

    def e_b3m(p, sl):
        reduce_copy(yb, sl, 256, B, to_y).wait_recv()
        add(sl, block_b(s, yy), B, [(r_ob, (s * 2 + yy) * B), (r_xb, yy * B), (r_yb, 0)])
        finals(p, sl, block_b(s, yy), 1)

    def e_b4m(p, sl):
        r0 = block_b(s, 1 - yy)
        arrived(p, sl, r0)
        forward(p, sl, r0, 2, to_x).start()
        forward(p, sl, r0, 3, to_io).start()

    def e_b5m(p, sl):
        r0 = block_b(1 - s, yy)
        arrived(p, sl, r0)
        forward(p, sl, r0, 4, to_io).start()

    def e_b6m(p, sl):
        r0 = block_b(1 - s, 1 - yy)
        arrived(p, sl, r0)
        forward(p, sl, r0, 5, to_io).start()

    def e_cm(p, sl):
        for b in range(2):
            arrived(p, sl, block_a(1 - yy, b))
        for k in range(2):
            local_final(p, sl, 0, k).wait()
        for k in range(6):
            send_final(p, sl, 0, k, to_y).wait_send()
            forward(p, sl, 0, k, to_y).wait_send()
        for kind, n in ((ya, 128), (xa, B), (xbl, 128), (yb, B)):
            reduce_copy(kind, sl, 0, n, to_y).wait_send()
        sibling(p).start()

    def e_ce(p, sl):
        for b in range(2):
            arrived(p, sl, block_a(1 - yy, b))
        for b in range(4):
            arrived(p, sl, 256 + b * B)
        for k in range(2):
            forward(p, sl, 0, k, to_y).wait_send()
        for kind, n in ((ya, 128), (ob, 256), (oa, 128)):
            reduce_copy(kind, sl, 0, n, to_y).wait_send()
        sibling(p).start()

    events = dict(A1e=(end, e_a1e), A1m=(mid, e_a1m), A2m=(mid, e_a2m), A3m=(mid, e_a3m), A3e=(end, e_a3e), A4e=(end, e_a4e),
                  B1m=(mid, e_b1m), B2m=(mid, e_b2m), B3m=(mid, e_b3m), B4m=(mid, e_b4m), B5m=(mid, e_b5m), B6m=(mid, e_b6m),
                  Ce=(end, e_ce), Cm=(mid, e_cm))

    def comm(it, j):
        for k in sorted(OFF, key=lambda k: -OFF[k]):
            if (OFF[k] + SLOTS - 1 - j) % SLOTS:
                continue
            p = it - LEAD - (OFF[k] + SLOTS - 1 - j) // SLOTS
            role, run = events[k]

            @pl.when((p >= 0) & (p < PAIRS) & role)
            def _():
                run(p, p % NS)

    x_copy(0).start()
    for c in w_copies(0):
        c.start()

    def body(it, _):
        for half in range(2):
            u = 2 * it + half
            for strip in range(2):
                @pl.when(it < PAIRS)
                def _():
                    if strip == 0:
                        if half == 0:
                            pl.when(it % LEAD == 0)(x_copy(0).wait)
                        for c in w_copies(u):
                            c.wait()

                        @pl.when(u + 1 < 2 * PAIRS)
                        def _():
                            for c in w_copies(u + 1):
                                c.start()
                    gate_up(u, strip)
                    if half == 1 and strip == 1:
                        pl.when((it % LEAD == LEAD - 1) & (it < PAIRS - 1))(lambda: x_copy(it // LEAD + 1).start())
                comm(it, half * 2 + strip)
        p, q = it - LEAD, it - LEAD + 1

        @pl.when((q >= 0) & (q < PAIRS))
        def _():
            wd_copy(0, 0, 0).wait()
            pl.when(q >= 1)(lambda: swap(q - 1).wait_send())
            term_for_other(q)
            pl.when(q >= 2)(lambda: pl.semaphore_wait(credit, 1))
            swap(q).start()

        @pl.when((q + 1 >= 0) & (q + 1 < PAIRS))
        def _():
            wd_copy(0, 1 - core, q + 1).start()
        comm(it, 4)

        @pl.when((p >= 0) & (p < PAIRS))
        def _():
            wd_copy(1, 0, 0).wait()
            swap(p).wait_recv()
            own_term(p, p % NS)

            @pl.when(p < PAIRS - 2)
            def _():
                pl.semaphore_signal(credit, inc=1, device_id=to_s, device_id_type=pl.DeviceIdType.MESH)
            first(p, p % NS)

        @pl.when((p + 1 >= 0) & (p + 1 < PAIRS))
        def _():
            wd_copy(1, core, p + 1).start()
        comm(it, 5)
        return 0

    lax.fori_loop(0, NIT, body, 0)
    swap(PAIRS - 1).wait_send()

    def last(p, _):
        sibling(p).wait()
        return 0

    lax.fori_loop(0, PAIRS, last, 0)


def solution(mesh):
    def step(x, w_gate, w_up, w_down):
        any_ = pl.BlockSpec(memory_space=pl.ANY)
        dma = pltpu.SemaphoreType.DMA
        flops = 6 * ROWS * D * HID
        return pl.pallas_call(
            kernel,
            out_shape=jax.ShapeDtypeStruct((ROWS, D), BF16),
            in_specs=[any_] * 4,
            out_specs=any_,
            scratch_shapes=[
                pltpu.VMEM((R, D), BF16),
                pltpu.VMEM((2, D, TN), BF16),
                pltpu.VMEM((2, D, TN), BF16),
                pltpu.VMEM((2, R, HID), BF16),
                pltpu.VMEM((2, HID, CW), BF16),
                pltpu.VMEM((R, CW), BF16),
                pltpu.VMEM((2, R, CW), BF16),
                pltpu.VMEM((NS, R, CW), F32),
                pltpu.VMEM((NS, R, CW), BF16),
                pltpu.VMEM((NS, 2 * B, CW), BF16),
                pltpu.VMEM((NS, 2 * B, CW), BF16),
                pltpu.VMEM((NS, B, CW), BF16),
                pltpu.VMEM((NS, 4 * B, CW), BF16),
                pltpu.VMEM((NS, 2 * B, CW), BF16),
                pltpu.VMEM((NS, B, CW), BF16),
                dma,
                dma((2, 2)),
                dma((2,)),
                dma,
                dma((2,)),
                pltpu.SemaphoreType.REGULAR,
                dma((NS, 6)),
                dma((NS, 6)),
                dma((NS, 8)),
                dma((1,)),
                dma((NS, 6)),
                dma((NS, 2)),
                dma((NS, 6)),
                dma((2, PAIRS)),
            ],
            compiler_params=pltpu.CompilerParams(
                collective_id=0, has_side_effects=True, vmem_limit_bytes=67043328),
            cost_estimate=pl.CostEstimate(flops=flops, bytes_accessed=1 << 29, transcendentals=ROWS * HID),
            name="mlp",
        )(x, w_gate, w_up, w_down)

    return jax.shard_map(
        step,
        mesh=mesh,
        in_specs=(P("dp", None), P(None, "tp"), P(None, "tp"), P("tp", None)),
        out_specs=P("dp", None),
        check_vma=False,
    )
```

time: 844 us -> 394 us (0.47)
  waiting for transfers between devices: 567 us -> 0 us
  Pallas kernels: 0 us -> 370 us
  matrix products: 240 us -> 0 us
  between operations: 13.4 us -> 0.01 us
    psum x1 -> x0, waiting for transfers between devices: 567 us -> none  [step(): return lax.psum(term, 'tp')]
    pallas_call x0 -> x1, Pallas kernels: none -> 370 us  [step(): pl.pallas_call(kernel, out_shape=jax.ShapeDtypeStruct((ROWS, D), BF16), i...]
    dot_general x3 -> x0, matrix products: 240 us -> none  [the longest x1 83.1 us: step(): up = jnp.dot(x, w_up, preferred_element_type=jnp.float32)]
  transfers between devices with their start and end apart: 1 -> 0, of which waited for: 1 -> 0; matrix products, arithmetic and copies ran while one was open for 0% -> 0% of each run, Pallas kernels for 0% -> 0%
where the time goes in v1:
time: 394 us; the launch traced here: 393 us
  Pallas kernels  370 us (94%)
  local copies, waits for them, and re-layouts  23 us (6%)
    pallas_call x1, Pallas kernels, step(): pl.pallas_call(kernel, out_shape=jax.ShapeDtypeStruct((ROWS, D), BF16), i...  370 us
    unnamed x1, local copies, waits for them, and re-layouts  23 us

profile of v1, /device:TPU:0, one launch (start us, length us, event | category | flops | bytes accessed | tf_op | source)
XLA Modules:
  0.0 393.5 jit_solution(10506395957389877283)
XLA Ops:
  0.0 370.5 %mlp.1 = bf16[2048,8192]{1,0:T(8,128)(2,1)} custom-call(bf16[2048,8192]{1,0:T(8,128)(2,1)} %x.1, bf16[8192,2048]{1,0:T(8,128)(2,1)} %wg.1, bf16[8192,2048]{1,0:T(8,128)(2,1)} %wu.1, bf16[2048,8192]{1,0:T(8,128)(2,1)} %wd.1), custom_call_target="tpu_custom_call" | custom-call | flops 206158430208 | bytes 536870912 | tf_op jit(solution)/shard_map/mlp/pallas_call | solution.py:322
  370.5 23.0 %copy.6 = bf16[2048,8192]{1,0:T(8,128)(2,1)} copy(bf16[2048,8192]{1,0:T(8,128)(2,1)} %mlp.1) | data formatting | bytes 67108864

commit v2 on v1

v2 whole, which is shorter than its diff:
```python
import jax
import jax.numpy as jnp
from jax import lax
from jax.experimental import pallas as pl
from jax.experimental.pallas import tpu as pltpu
from jax.sharding import PartitionSpec as P

ROWS, D, HID = 2048, 8192, 2048
R = 512
CW = 512
HALF = D // 2
NQ = HALF // CW
CHUNKS = ROWS // R
PAIRS = CHUNKS * NQ
TN = 256
UNITS = HID // TN
NS = 8
B = 64
SLOTS = 4
LEAD = UNITS
OFF = dict(Cm=29, B5m=20, A1e=3, B1m=7, A1m=8, A3e=15, A3m=20, B4m=20, B8e=22, Ce=28, B2m=11, A2m=13, A4e=22, B3m=14, B7e=16)
NIT = LEAD + PAIRS + max(OFF.values()) // SLOTS
F32, BF16 = jnp.float32, jnp.bfloat16


def kernel(x, wg, wu, wd, y, xb, gb, ub, hb, wdb, dsend, drecv, sf, sb, r_ya, r_oa, r_xa, r_ob, r_xb, r_yb,
           s_x, s_w, s_wd, s_ds, s_dr, credit, q_rs, q_send, q_final, q_leaf, q_sib):
    dp, t = lax.axis_index("dp"), lax.axis_index("tp")
    core, z, yy = t % 2, (t // 2) % 4, t // 8
    s = z // 2
    mid = (z == 1) | (z == 2)
    end = (z == 0) | (z == 3)

    def tid(a, b, c):
        return (dp, (a * 4 + b) * 2 + c)

    to_y, to_x, to_s = tid(1 - yy, z, core), tid(yy, 3 - z, core), tid(yy, z, 1 - core)
    to_io = tid(yy, z + 1 - 2 * (z % 2), core)

    def rcopy(src, dst, ssem, rsem, dev):
        return pltpu.make_async_remote_copy(
            src_ref=src, dst_ref=dst, send_sem=ssem, recv_sem=rsem, device_id=dev, device_id_type=pl.DeviceIdType.MESH)

    bar = pltpu.get_barrier_semaphore()
    for dev in (to_y, to_io, to_s):
        pl.semaphore_signal(bar, inc=1, device_id=dev, device_id_type=pl.DeviceIdType.MESH)

    @pl.when(mid)
    def _():
        pl.semaphore_signal(bar, inc=1, device_id=to_x, device_id_type=pl.DeviceIdType.MESH)
        pl.semaphore_wait(bar, 4)

    @pl.when(end)
    def _():
        pl.semaphore_wait(bar, 3)

    def rows(r0, n):
        return pl.ds(pl.multiple_of(r0, B), n)

    def x_copy(c, i):
        h = R // 2
        return pltpu.make_async_copy(x.at[rows(c * R + i * h, h), :], xb.at[pl.ds(i * h, h), :], s_x.at[i])

    def w_copies(u):
        b, n = u % 2, pl.ds(pl.multiple_of((u % UNITS) * TN, TN), TN)
        return (pltpu.make_async_copy(wg.at[:, n], gb.at[b], s_w.at[b, 0]),
                pltpu.make_async_copy(wu.at[:, n], ub.at[b], s_w.at[b, 1]))

    def wd_copy(k, half, p):
        n = pl.ds(pl.multiple_of(half * HALF + (p % NQ) * CW, CW), CW)
        return pltpu.make_async_copy(wd.at[:, n], wdb.at[k], s_wd.at[k])

    def gate_up(u, i):
        b, n = u % 2, pl.ds(pl.multiple_of((u % UNITS) * TN, TN), TN)
        r = pl.ds(i * (R // 2), R // 2)
        g = jnp.dot(xb[r, :], gb[b], preferred_element_type=F32)
        up = jnp.dot(xb[r, :], ub[b], preferred_element_type=F32)
        hb[(u // UNITS) % 2, r, n] = (jax.nn.silu(g) * up).astype(BF16)

    def swap(q):
        return rcopy(dsend, drecv.at[q % 2], s_ds, s_dr.at[q % 2], to_s)

    def term_for_other(q):
        for j in range(1):
            n = pl.ds(j * CW, CW)
            dsend[:, n] = jnp.dot(hb[(q // NQ) % 2], wdb[0, :, n], preferred_element_type=F32).astype(BF16)

    def own_term(p, sl):
        for j in range(1):
            n = pl.ds(j * CW, CW)
            v = jnp.dot(hb[(p // NQ) % 2], wdb[1, :, n], preferred_element_type=F32) + drecv[p % 2, :, n].astype(F32)
            sf[sl, :, n] = v
            sb[sl, :, n] = v.astype(BF16)

    def add(sl, r0, n, srcs):
        w = 32
        def strip(i, _):
            v = sf[sl, pl.ds(pl.multiple_of(r0 + i * w, w), w), :]
            for ref, q0 in srcs:
                v = v + ref[sl, pl.ds(pl.multiple_of(q0 + i * w, w), w), :].astype(F32)
            sb[sl, pl.ds(pl.multiple_of(r0 + i * w, w), w), :] = v.astype(BF16)
            return 0
        lax.fori_loop(0, n // w, strip, 0, unroll=True)

    ya, oa, xa, ob, xbl, yb = range(6)

    def reduce_copy(kind, sl, r0, n, dev):
        dst = (r_ya, r_oa, r_xa, r_ob, r_xb, r_yb)[kind].at[sl]
        return rcopy(sb.at[sl, rows(r0, n), :], dst, q_send.at[sl], q_rs.at[sl, kind], dev)

    def y_at(p, r0, n):
        col = pl.multiple_of(core * HALF + (p % NQ) * CW, CW)
        return y.at[rows((p // NQ) * R + r0, n), pl.ds(col, CW)]

    def block_a(a, b):
        return (a * 2 + b) * B

    def block_b(b, a):
        return 256 + (b * 2 + a) * B

    def final_sem(sl, r0):
        return q_final.at[sl, r0 // B]

    def local_final(p, sl, r0):
        return pltpu.make_async_copy(sb.at[sl, rows(r0, B), :], y_at(p, r0, B), q_send.at[sl])

    def send_final(p, sl, r0, dev, leaf=False):
        sem = q_leaf.at[sl] if leaf else final_sem(sl, r0)
        return rcopy(sb.at[sl, rows(r0, B), :], y_at(p, r0, B), q_send.at[sl], sem, dev)

    def forward(p, sl, r0, dev, leaf=False):
        sem = q_leaf.at[sl] if leaf else final_sem(sl, r0)
        return rcopy(y_at(p, r0, B), y_at(p, r0, B), q_send.at[sl], sem, dev)

    def wait_blocks(sem, n):
        part = y.at[pl.ds(0, n * B), pl.ds(0, CW)]
        pltpu.make_async_copy(part, part, sem).wait()

    def sibling(p):
        return rcopy(y_at(p, 0, R), y_at(p, 0, R), q_sib.at[0, p], q_sib.at[1, p], to_s)

    def first(p, sl):
        reduce_copy(ya, sl, (1 - yy) * 128, 128, to_y).start()

        @pl.when(end)
        def _():
            reduce_copy(ob, sl, 256, 256, to_io).start()

    def e_a1e(p, sl):
        reduce_copy(ya, sl, 0, 128, to_y).wait_recv()
        add(sl, yy * 128, 128, [(r_ya, 0)])
        reduce_copy(oa, sl, yy * 128, 128, to_io).start()

    def e_a1m(p, sl):
        reduce_copy(ya, sl, 0, 128, to_y).wait_recv()
        reduce_copy(oa, sl, 0, 128, to_io).wait_recv()
        add(sl, block_a(yy, 1 - s), B, [(r_ya, (1 - s) * B), (r_oa, (1 - s) * B)])
        reduce_copy(xa, sl, block_a(yy, 1 - s), B, to_x).start()

    def finals(p, sl, r0, leaf):
        send_final(p, sl, r0, to_x).start()
        send_final(p, sl, r0, to_io).start()
        send_final(p, sl, r0, to_y, leaf).start()
        local_final(p, sl, r0).start()

    def e_a2m(p, sl):
        reduce_copy(xa, sl, 0, B, to_x).wait_recv()
        add(sl, block_a(yy, s), B, [(r_ya, s * B), (r_oa, s * B), (r_xa, 0)])
        finals(p, sl, block_a(yy, s), True)

    def arrived(p, sl, r0):
        forward(p, sl, r0, to_y).wait_recv()

    def e_a3m(p, sl):
        r0 = block_a(yy, 1 - s)
        arrived(p, sl, r0)
        forward(p, sl, r0, to_io).start()
        forward(p, sl, r0, to_y, True).start()

    def pass_across(r0):
        def run(p, sl):
            arrived(p, sl, r0)
            forward(p, sl, r0, to_y, True).start()
        return run

    e_a3e, e_a4e = pass_across(block_a(yy, s)), pass_across(block_a(yy, 1 - s))
    e_b7e, e_b8e = pass_across(block_b(s, yy)), pass_across(block_b(1 - s, yy))

    def e_b1m(p, sl):
        reduce_copy(ob, sl, 256, 256, to_io).wait_recv()
        add(sl, block_b(1 - s, 0), 128, [(r_ob, (1 - s) * 128)])
        reduce_copy(xbl, sl, block_b(1 - s, 0), 128, to_x).start()

    def e_b2m(p, sl):
        reduce_copy(xbl, sl, 256, 128, to_x).wait_recv()
        add(sl, block_b(s, 1 - yy), B, [(r_ob, (s * 2 + 1 - yy) * B), (r_xb, (1 - yy) * B)])
        reduce_copy(yb, sl, block_b(s, 1 - yy), B, to_y).start()

    def e_b3m(p, sl):
        reduce_copy(yb, sl, 256, B, to_y).wait_recv()
        add(sl, block_b(s, yy), B, [(r_ob, (s * 2 + yy) * B), (r_xb, yy * B), (r_yb, 0)])
        finals(p, sl, block_b(s, yy), False)

    def e_b4m(p, sl):
        r0 = block_b(s, 1 - yy)
        arrived(p, sl, r0)
        forward(p, sl, r0, to_x, True).start()

    def e_b5m(p, sl):
        r0 = block_b(1 - s, yy)
        arrived(p, sl, r0)
        forward(p, sl, r0, to_io).start()

    def e_cm(p, sl):
        wait_blocks(q_leaf.at[sl], 3)
        wait_blocks(q_send.at[sl], 18)
        sibling(p).start()

    def e_ce(p, sl):
        wait_blocks(q_leaf.at[sl], 4)
        wait_blocks(q_send.at[sl], 12)
        sibling(p).start()

    events = dict(A1e=(end, e_a1e), A1m=(mid, e_a1m), A2m=(mid, e_a2m), A3m=(mid, e_a3m), A3e=(end, e_a3e), A4e=(end, e_a4e),
                  B1m=(mid, e_b1m), B2m=(mid, e_b2m), B3m=(mid, e_b3m), B4m=(mid, e_b4m), B5m=(mid, e_b5m), B7e=(end, e_b7e), B8e=(end, e_b8e),
                  Ce=(end, e_ce), Cm=(mid, e_cm))

    def comm(it, j):
        here = [(OFF[k], OFF[k] // SLOTS, *events[k]) for k in sorted(OFF, key=lambda k: -OFF[k]) if OFF[k] % SLOTS == j]
        if not here:
            return
        lags = [e[1] for e in here]
        steady = (it >= LEAD + max(lags)) & (it < LEAD + PAIRS + min(lags))

        def run_all(role, guarded):
            for _, lag, of, run in here:
                if of is not role:
                    continue
                p = it - LEAD - lag
                if guarded:
                    pl.when((p >= 0) & (p < PAIRS))(lambda run=run, p=p: run(p, p % NS))
                else:
                    run(p, p % NS)

        def both(guarded):
            lax.cond(mid, lambda: run_all(mid, guarded), lambda: run_all(end, guarded))

        lax.cond(steady, lambda: both(False), lambda: both(True))

    x_copy(0, 0).start()
    for c in w_copies(0):
        c.start()
    x_copy(0, 1).start()

    def other_half(q):
        wd_copy(0, 0, 0).wait()
        pl.when(q >= 1)(lambda: swap(q - 1).wait_send())
        term_for_other(q)
        pl.when(q >= 2)(lambda: pl.semaphore_wait(credit, 1))
        swap(q).start()
        pl.when(q + 1 < PAIRS)(lambda: wd_copy(0, 1 - core, q + 1).start())

    def body(it, _):
        p, q = it - LEAD, it - LEAD + 1

        @pl.when((p >= 0) & (p < PAIRS))
        def _():
            wd_copy(1, 0, 0).wait()
            swap(p).wait_recv()
            own_term(p, p % NS)

            @pl.when(p < PAIRS - 2)
            def _():
                pl.semaphore_signal(credit, inc=1, device_id=to_s, device_id_type=pl.DeviceIdType.MESH)
            first(p, p % NS)
            pl.when(p + 1 < PAIRS)(lambda: wd_copy(1, core, p + 1).start())
        comm(it, 0)
        pl.when((q >= 1) & (q < PAIRS) & (q % NQ != 0))(lambda: other_half(q))
        comm(it, 1)
        for i in range(2):
            @pl.when(it < PAIRS)
            def _():
                pl.when(it % UNITS == 0)(x_copy(0, i).wait)
                if i == 0:
                    for c in w_copies(it):
                        c.wait()

                    @pl.when(it + 1 < PAIRS)
                    def _():
                        for c in w_copies(it + 1):
                            c.start()

                    @pl.when(it == 0)
                    def _():
                        wd_copy(0, 1 - core, 0).start()
                        wd_copy(1, core, 0).start()
                gate_up(it, i)
                pl.when((it % UNITS == UNITS - 1) & (it < PAIRS - 1))(lambda: x_copy(it // UNITS + 1, i).start())
            comm(it, 2 + i)
        pl.when((q >= 0) & (q < PAIRS) & (q % NQ == 0))(lambda: other_half(q))
        return 0

    lax.fori_loop(0, NIT, body, 0)
    swap(PAIRS - 1).wait_send()

    def last(p, _):
        sibling(p).wait()
        return 0

    lax.fori_loop(0, PAIRS, last, 0)


def copy_out(a, o, buf, si, so):
    n, r, steps = 8, ROWS // 16, 16

    def load(i):
        return pltpu.make_async_copy(a.at[pl.ds(i * r, r), :], buf.at[i % n], si.at[i % n])

    def store(i):
        return pltpu.make_async_copy(buf.at[i % n], o.at[pl.ds(i * r, r), :], so.at[i % n])

    for i in range(n // 2):
        load(i).start()
    for i in range(steps):
        load(i).wait()
        store(i).start()
        j = i + n // 2
        if j < steps:
            if j >= n:
                store(j - n).wait()
            load(j).start()
    for i in range(steps - n, steps):
        store(i).wait()


def solution(mesh):
    def step(x, w_gate, w_up, w_down):
        any_ = pl.BlockSpec(memory_space=pl.ANY)
        dma = pltpu.SemaphoreType.DMA
        flops = 6 * ROWS * D * HID
        y = pl.pallas_call(
            kernel,
            out_shape=jax.ShapeDtypeStruct((ROWS, D), BF16),
            in_specs=[any_] * 4,
            out_specs=any_,
            scratch_shapes=[
                pltpu.VMEM((R, D), BF16),
                pltpu.VMEM((2, D, TN), BF16),
                pltpu.VMEM((2, D, TN), BF16),
                pltpu.VMEM((2, R, HID), BF16),
                pltpu.VMEM((2, HID, CW), BF16),
                pltpu.VMEM((R, CW), BF16),
                pltpu.VMEM((2, R, CW), BF16),
                pltpu.VMEM((NS, R, CW), F32),
                pltpu.VMEM((NS, R, CW), BF16),
                pltpu.VMEM((NS, 2 * B, CW), BF16),
                pltpu.VMEM((NS, 2 * B, CW), BF16),
                pltpu.VMEM((NS, B, CW), BF16),
                pltpu.VMEM((NS, 4 * B, CW), BF16),
                pltpu.VMEM((NS, 2 * B, CW), BF16),
                pltpu.VMEM((NS, B, CW), BF16),
                dma((2,)),
                dma((2, 2)),
                dma((2,)),
                dma,
                dma((2,)),
                pltpu.SemaphoreType.REGULAR,
                dma((NS, 6)),
                dma((NS,)),
                dma((NS, 8)),
                dma((NS,)),
                dma((2, PAIRS)),
            ],
            compiler_params=pltpu.CompilerParams(
                collective_id=0, has_side_effects=True, vmem_limit_bytes=67043328),
            cost_estimate=pl.CostEstimate(flops=flops, bytes_accessed=1 << 29, transcendentals=ROWS * HID),
            name="mlp",
        )(x, w_gate, w_up, w_down)
        return pl.pallas_call(
            copy_out,
            out_shape=jax.ShapeDtypeStruct((ROWS, D), BF16),
            in_specs=[any_],
            out_specs=any_,
            scratch_shapes=[pltpu.VMEM((8, ROWS // 16, D), BF16), dma((8,)), dma((8,))],
            compiler_params=pltpu.CompilerParams(vmem_limit_bytes=60 << 20),
            cost_estimate=pl.CostEstimate(flops=0, bytes_accessed=4 * ROWS * D, transcendentals=0),
            name="copy_out",
        )(y)

    return jax.shard_map(
        step,
        mesh=mesh,
        in_specs=(P("dp", None), P(None, "tp"), P(None, "tp"), P("tp", None)),
        out_specs=P("dp", None),
        check_vma=False,
    )
```

time: 394 us -> 374 us (0.949)
  local copies, waits for them, and re-layouts: 23 us -> 0 us
  Pallas kernels: 370 us -> 374 us
    unnamed x1 -> x0, local copies, waits for them, and re-layouts: 23 us -> none
    pallas_call x0 -> x1, Pallas kernels: none -> 22 us  [step(): pl.pallas_call(copy_out, out_shape=jax.ShapeDtypeStruct((ROWS, D), BF16),...]
    pallas_call x1, Pallas kernels: 370 us -> 352 us  [step(): pl.pallas_call(kernel, out_shape=jax.ShapeDtypeStruct((ROWS, D), BF16), i...]
where the time goes in v2:
time: 374 us
  Pallas kernels  374 us (100%)
    pallas_call x1, Pallas kernels, step(): pl.pallas_call(kernel, out_shape=jax.ShapeDtypeStruct((ROWS, D), BF16), i...  352 us
    pallas_call x1, Pallas kernels, step(): pl.pallas_call(copy_out, out_shape=jax.ShapeDtypeStruct((ROWS, D), BF16),...  22 us

profile of v2, /device:TPU:0, one launch (start us, length us, event | category | flops | bytes accessed | tf_op | source)
XLA Modules:
  0.0 374.2 jit_solution(4414159692474652378)
XLA Ops:
  0.0 352.1 %mlp.1.a = bf16[2048,8192]{1,0:T(8,128)(2,1)} custom-call(bf16[2048,8192]{1,0:T(8,128)(2,1)} %x.1, bf16[8192,2048]{1,0:T(8,128)(2,1)} %wg.1, bf16[8192,2048]{1,0:T(8,128)(2,1)} %wu.1, bf16[2048,8192]{1,0:T(8,128)(2,1)} %wd.1), custom_call_target="tpu_custom_call" | custom-call | flops 206158430208 | bytes 536870912 | tf_op jit(solution)/shard_map/mlp/pallas_call | solution.py:341
  352.1 22.0 %copy_out.1 = bf16[2048,8192]{1,0:T(8,128)(2,1)} custom-call(bf16[2048,8192]{1,0:T(8,128)(2,1)} %mlp.1.a), custom_call_target="tpu_custom_call" | custom-call | bytes 67108864 | tf_op jit(solution)/shard_map/copy_out/pallas_call | solution.py:379

commit v3 on v2

--- a/solution.py
+++ b/solution.py
@@ -20,11 +20,12 @@
 LEAD = UNITS
 OFF = dict(Cm=29, B5m=20, A1e=3, B1m=7, A1m=8, A3e=15, A3m=20, B4m=20, B8e=22, Ce=28, B2m=11, A2m=13, A4e=22, B3m=14, B7e=16)
 NIT = LEAD + PAIRS + max(OFF.values()) // SLOTS
+KEEP = NIT - 7
 F32, BF16 = jnp.float32, jnp.bfloat16
 
 
 def kernel(x, wg, wu, wd, y, xb, gb, ub, hb, wdb, dsend, drecv, sf, sb, r_ya, r_oa, r_xa, r_ob, r_xb, r_yb,
-           s_x, s_w, s_wd, s_ds, s_dr, credit, q_rs, q_send, q_final, q_leaf, q_sib):
+           s_x, s_w, s_wd, s_ds, s_dr, credit, q_rs, q_send, q_final, q_leaf, q_sib, s_keep):
     dp, t = lax.axis_index("dp"), lax.axis_index("tp")
     core, z, yy = t % 2, (t // 2) % 4, t // 8
     s = z // 2
@@ -260,8 +261,22 @@
         swap(q).start()
         pl.when(q + 1 < PAIRS)(lambda: wd_copy(0, 1 - core, q + 1).start())
 
+    def landed(p, _):
+        sibling(p).wait_recv()
+        return 0
+
     def body(it, _):
         p, q = it - LEAD, it - LEAD + 1
+
+        @pl.when(it == KEEP)
+        def _():
+            lax.fori_loop(0, 3 * NQ, landed, 0)
+            pltpu.make_async_copy(y.at[pl.ds(0, R), :], xb, s_keep.at[0]).start()
+            for c, ref in ((1, gb), (2, ub)):
+                for k in range(D // TN // 2):
+                    for src, dst in kept(y, ref, k, c):
+                        pltpu.make_async_copy(src, dst, s_keep.at[c]).start()
+
 
         @pl.when((p >= 0) & (p < PAIRS))
         def _():
@@ -303,50 +318,69 @@
     lax.fori_loop(0, NIT, body, 0)
     swap(PAIRS - 1).wait_send()
 
+    pltpu.make_async_copy(y.at[pl.ds(0, R), :], xb, s_keep.at[0]).wait()
+    for c in (1, 2):
+        pltpu.make_async_copy(y.at[pl.ds(c * R, R), :], y.at[pl.ds(c * R, R), :], s_keep.at[c]).wait()
+
     def last(p, _):
-        sibling(p).wait()
+        sibling(p).wait_send()
+        pl.when(p >= 3 * NQ)(sibling(p).wait_recv)
         return 0
 
     lax.fori_loop(0, PAIRS, last, 0)
 
 
-def copy_out(a, o, buf, si, so):
-    n, r, steps = 8, ROWS // 16, 16
+def kept(y, ref, k, c):
+    for half in range(2):
+        col = (half * (D // TN // 2) + k) * TN
+        yield y.at[pl.ds(c * R, R), pl.ds(col, TN)], ref.at[half, pl.ds(k * R, R), :]
+
+
+def copy_out(a, ra, rb, rc, o, buf, si, so, sk):
+    n, r, steps = 4, 128, R // 128
+    base = 3 * R
 
     def load(i):
-        return pltpu.make_async_copy(a.at[pl.ds(i * r, r), :], buf.at[i % n], si.at[i % n])
+        return pltpu.make_async_copy(a.at[pl.ds(base + i * r, r), :], buf.at[i % n], si.at[i % n])
 
     def store(i):
-        return pltpu.make_async_copy(buf.at[i % n], o.at[pl.ds(i * r, r), :], so.at[i % n])
-
-    for i in range(n // 2):
+        return pltpu.make_async_copy(buf.at[i % n], o.at[pl.ds(base + i * r, r), :], so.at[i % n])
+
+    for i in range(steps):
         load(i).start()
+    whole = pltpu.make_async_copy(ra, o.at[pl.ds(0, R), :], sk.at[0])
+    whole.start()
+    for c, ref in ((1, rb), (2, rc)):
+        for k in range(D // TN // 2):
+            for dst, src in kept(o, ref, k, c):
+                pltpu.make_async_copy(src, dst, sk.at[c]).start()
     for i in range(steps):
         load(i).wait()
         store(i).start()
-        j = i + n // 2
-        if j < steps:
-            if j >= n:
-                store(j - n).wait()
-            load(j).start()
-    for i in range(steps - n, steps):
+    for i in range(steps):
         store(i).wait()
+    whole.wait()
+    for c in (1, 2):
+        pltpu.make_async_copy(o.at[pl.ds(c * R, R), :], o.at[pl.ds(c * R, R), :], sk.at[c]).wait()
 
 
 def solution(mesh):
     def step(x, w_gate, w_up, w_down):
         any_ = pl.BlockSpec(memory_space=pl.ANY)
         dma = pltpu.SemaphoreType.DMA
+        vmem = pl.BlockSpec(memory_space=pltpu.VMEM)
         flops = 6 * ROWS * D * HID
-        y = pl.pallas_call(
+        y, rows_a, rows_b, rows_c = pl.pallas_call(
             kernel,
-            out_shape=jax.ShapeDtypeStruct((ROWS, D), BF16),
-            in_specs=[any_] * 4,
-            out_specs=any_,
-            scratch_shapes=[
+            out_shape=(
+                jax.ShapeDtypeStruct((ROWS, D), BF16),
                 pltpu.VMEM((R, D), BF16),
                 pltpu.VMEM((2, D, TN), BF16),
                 pltpu.VMEM((2, D, TN), BF16),
+            ),
+            in_specs=[any_] * 4,
+            out_specs=(any_, vmem, vmem, vmem),
+            scratch_shapes=[
                 pltpu.VMEM((2, R, HID), BF16),
                 pltpu.VMEM((2, HID, CW), BF16),
                 pltpu.VMEM((R, CW), BF16),
@@ -370,22 +404,23 @@
                 dma((NS, 8)),
                 dma((NS,)),
                 dma((2, PAIRS)),
+                dma((3,)),
             ],
             compiler_params=pltpu.CompilerParams(
-                collective_id=0, has_side_effects=True, vmem_limit_bytes=67043328),
+                collective_id=0, has_side_effects=True, vmem_limit_bytes=38 << 20),
             cost_estimate=pl.CostEstimate(flops=flops, bytes_accessed=1 << 29, transcendentals=ROWS * HID),
             name="mlp",
         )(x, w_gate, w_up, w_down)
         return pl.pallas_call(
             copy_out,
             out_shape=jax.ShapeDtypeStruct((ROWS, D), BF16),
-            in_specs=[any_],
+            in_specs=[any_, vmem, vmem, vmem],
             out_specs=any_,
-            scratch_shapes=[pltpu.VMEM((8, ROWS // 16, D), BF16), dma((8,)), dma((8,))],
-            compiler_params=pltpu.CompilerParams(vmem_limit_bytes=60 << 20),
-            cost_estimate=pl.CostEstimate(flops=0, bytes_accessed=4 * ROWS * D, transcendentals=0),
+            scratch_shapes=[pltpu.VMEM((4, 128, D), BF16), dma((4,)), dma((4,)), dma((3,))],
+            compiler_params=pltpu.CompilerParams(vmem_limit_bytes=10 << 20),
+            cost_estimate=pl.CostEstimate(flops=0, bytes_accessed=3 * ROWS * D, transcendentals=0),
             name="copy_out",
-        )(y)
+        )(y, rows_a, rows_b, rows_c)
 
     return jax.shard_map(
         step,

time: 374 us -> 365 us (0.976)
  Pallas kernels: 374 us -> 364 us
    pallas_call x1, Pallas kernels: 22 us -> 13.4 us  [step(): pl.pallas_call(copy_out, out_shape=jax.ShapeDtypeStruct((ROWS, D), BF16),...]
where the time goes in v3:
time: 365 us
  Pallas kernels  364 us (100%)
    pallas_call x1, Pallas kernels, step(): pl.pallas_call(kernel, out_shape=(jax.ShapeDtypeStruct((ROWS, D), BF16),...  351 us
    pallas_call x1, Pallas kernels, step(): pl.pallas_call(copy_out, out_shape=jax.ShapeDtypeStruct((ROWS, D), BF16),...  13.4 us

profile of v3, /device:TPU:0, one launch (start us, length us, event | category | flops | bytes accessed | tf_op | source)
XLA Modules:
  0.0 364.5 jit_solution(6644253588723201743)
XLA Ops:
  0.0 351.1 %mlp.1 = (bf16[2048,8192]{1,0:T(8,128)(2,1)}, bf16[512,8192]{1,0:T(8,128)(2,1)S(1)}, bf16[2,8192,256]{2,1,0:T(8,128)(2,1)S(1)}, bf16[2,8192,256]{2,1,0:T(8,128)(2,1)S(1)}) custom-call(bf16[2048,8192]{1,0:T(8,128)(2,1)} %x.1, bf16[8192,2048]{1,0:T(8,128)(2,1)} %wg.1, bf16[8192,2048]{1,0:T(8,128)(2,1)} %wu.1, bf16[2048,8192]{1,0:T(8,128)(2,1)} %wd.1), custom_call_target="tpu_custom_call" | custom-call | flops 206158430208 | bytes 536870912 | tf_op jit(solution)/shard_map/mlp/pallas_call | solution.py:373
  351.1 13.4 %copy_out.1 = bf16[2048,8192]{1,0:T(8,128)(2,1)} custom-call(bf16[2048,8192]{1,0:T(8,128)(2,1)} %get-tuple-element.9.a, bf16[512,8192]{1,0:T(8,128)(2,1)S(1)} %get-tuple-element.10.ra, bf16[2,8192,256]{2,1,0:T(8,128)(2,1)S(1)} %get-tuple-element.11.rb, bf16[2,8192,256]{2,1,0:T(8,128)(2,1)S(1)} %get-tuple-element.12.rc), custom_call_target="tpu_custom_call" | custom-call | bytes 50331648 | tf_op jit(solution)/shard_map/copy_out/pallas_call | solution.py:414

commit v4 on v3

--- a/solution.py
+++ b/solution.py
@@ -103,10 +103,13 @@
             return 0
         lax.fori_loop(0, n // w, strip, 0, unroll=True)
 
-    ya, oa, xa, ob, xbl, yb = range(6)
+    ya, oa, xa, ob, xbl, yb, ob2 = range(7)
 
     def reduce_copy(kind, sl, r0, n, dev):
-        dst = (r_ya, r_oa, r_xa, r_ob, r_xb, r_yb)[kind].at[sl]
+        if kind in (ob, ob2):
+            dst = r_ob.at[sl, rows((1 - s if kind == ob else s) * 2 * B, 2 * B), :]
+        else:
+            dst = (r_ya, r_oa, r_xa, None, r_xb, r_yb)[kind].at[sl]
         return rcopy(sb.at[sl, rows(r0, n), :], dst, q_send.at[sl], q_rs.at[sl, kind], dev)
 
     def y_at(p, r0, n):
@@ -145,7 +148,8 @@
 
         @pl.when(end)
         def _():
-            reduce_copy(ob, sl, 256, 256, to_io).start()
+            reduce_copy(ob, sl, block_b(1 - s, 0), 128, to_io).start()
+            reduce_copy(ob2, sl, block_b(s, 0), 128, to_io).start()
 
     def e_a1e(p, sl):
         reduce_copy(ya, sl, 0, 128, to_y).wait_recv()
@@ -188,11 +192,12 @@
     e_b7e, e_b8e = pass_across(block_b(s, yy)), pass_across(block_b(1 - s, yy))
 
     def e_b1m(p, sl):
-        reduce_copy(ob, sl, 256, 256, to_io).wait_recv()
+        reduce_copy(ob, sl, 256, 128, to_io).wait_recv()
         add(sl, block_b(1 - s, 0), 128, [(r_ob, (1 - s) * 128)])
         reduce_copy(xbl, sl, block_b(1 - s, 0), 128, to_x).start()
 
     def e_b2m(p, sl):
+        reduce_copy(ob2, sl, 256, 128, to_io).wait_recv()
         reduce_copy(xbl, sl, 256, 128, to_x).wait_recv()
         add(sl, block_b(s, 1 - yy), B, [(r_ob, (s * 2 + 1 - yy) * B), (r_xb, (1 - yy) * B)])
         reduce_copy(yb, sl, block_b(s, 1 - yy), B, to_y).start()
@@ -399,7 +404,7 @@
                 dma,
                 dma((2,)),
                 pltpu.SemaphoreType.REGULAR,
-                dma((NS, 6)),
+                dma((NS, 7)),
                 dma((NS,)),
                 dma((NS, 8)),
                 dma((NS,)),

time: 365 us -> 364 us (level)
  no operation moved by 1% of the time
where the time goes in v4:
time: 364 us
  Pallas kernels  364 us (100%)
    pallas_call x1, Pallas kernels, step(): pl.pallas_call(kernel, out_shape=(jax.ShapeDtypeStruct((ROWS, D), BF16),...  351 us
    pallas_call x1, Pallas kernels, step(): pl.pallas_call(copy_out, out_shape=jax.ShapeDtypeStruct((ROWS, D), BF16),...  13.4 us

profile of v4, /device:TPU:0, one launch (start us, length us, event | category | flops | bytes accessed | tf_op | source)
XLA Modules:
  0.0 364.0 jit_solution(11483333376737436820)
XLA Ops:
  0.0 350.6 %mlp.1 = (bf16[2048,8192]{1,0:T(8,128)(2,1)}, bf16[512,8192]{1,0:T(8,128)(2,1)S(1)}, bf16[2,8192,256]{2,1,0:T(8,128)(2,1)S(1)}, bf16[2,8192,256]{2,1,0:T(8,128)(2,1)S(1)}) custom-call(bf16[2048,8192]{1,0:T(8,128)(2,1)} %x.1, bf16[8192,2048]{1,0:T(8,128)(2,1)} %wg.1, bf16[8192,2048]{1,0:T(8,128)(2,1)} %wu.1, bf16[2048,8192]{1,0:T(8,128)(2,1)} %wd.1), custom_call_target="tpu_custom_call" | custom-call | flops 206158430208 | bytes 536870912 | tf_op jit(solution)/shard_map/mlp/pallas_call | solution.py:378
  350.6 13.4 %copy_out.1 = bf16[2048,8192]{1,0:T(8,128)(2,1)} custom-call(bf16[2048,8192]{1,0:T(8,128)(2,1)} %get-tuple-element.9.a, bf16[512,8192]{1,0:T(8,128)(2,1)S(1)} %get-tuple-element.10.ra, bf16[2,8192,256]{2,1,0:T(8,128)(2,1)S(1)} %get-tuple-element.11.rb, bf16[2,8192,256]{2,1,0:T(8,128)(2,1)S(1)} %get-tuple-element.12.rc), custom_call_target="tpu_custom_call" | custom-call | bytes 50331648 | tf_op jit(solution)/shard_map/copy_out/pallas_call | solution.py:419
